TPU v7x, 32 devices: a whole 2x2x4 slice. The times are simulated.
32 devices in a mesh: wa: 16 (over z, y, core), ha: 2 (over x).
Axes of the slice: x: 2, y: 2, z: 4, core: 2. Of those that a mesh axis runs over, the one named last changes fastest.
Arguments:
- tokens: bfloat16 [16384, 4096], P('wa'), may hold values from -6 to 6
- expert_ids: int32 [16384, 8], P('wa'), may hold values from 0 to 127, as said below
- keep_mask: int32 [16384, 8], P('wa'), may hold values from 0 to 1, as said below
- route_weight: float32 [16384, 8], P('wa'), may hold values from 0.2 to 1
- gate_weight: bfloat16 [4096, 1536], P('wa', 'ha'), may hold values from -0.09375 to 0.09375
- up_weight: bfloat16 [4096, 1536], P('wa', 'ha'), may hold values from -0.09375 to 0.09375
- down_weight: bfloat16 [4096, 1536], P('wa', 'ha'), may hold values from -0.15625 to 0.15625
Outputs:
- mixed: bfloat16 [16384, 4096], P('wa', 'ha')
Inputs may be any that keep to these rules, and one draw needn't show every extreme that they name: `expert_ids`: each row names 8 different experts. keep_mask[t, k] is 1 exactly where fewer than 128 earlier tokens of the same block of 1024 rows name expert_ids[t, k]; in some block 128 tokens naming expert 0 are kept.
All inputs are finite; a program needn't handle non-finite values.
Results may differ from a plain program's by a relative error of at most 0.005.
Values may be sent and summed in bfloat16 or wider, within the bound.
A program may use at most 128 MiB of HBM per device.

v0:
```python
import jax
import jax.numpy as jnp
from jax import lax
from jax.sharding import PartitionSpec as P

CAP = 128


def prefix(value, axis, join, neutral):
    count, mine = (lax.axis_size(axis), lax.axis_index(axis))
    pieces = lax.all_gather(value, axis)
    subtotal = jnp.full_like(value, 0) + jnp.asarray(neutral, value.dtype)

    def turn(position, subtotal):
        longer = join(subtotal, pieces[position])
        return jnp.where(position < mine, longer, subtotal)

    return lax.fori_loop(0, count - 1, turn, subtotal)


def add_counts(earlier, later):
    return earlier + later


def global_admit(chosen, position):
    counted = jnp.sum(chosen).reshape(1)
    earlier = prefix(counted, "wa", add_counts, jnp.zeros((1,), jnp.int32))
    capacity = lax.axis_size("wa") * CAP // 2
    return chosen * (earlier[0] + position < capacity).astype(jnp.int32)


def slot_table(position, marked):
    slot_ids = jnp.arange(CAP, dtype=jnp.int32)
    return (position[None, :] == slot_ids[:, None]) & (marked[None, :] == 1)


def run_expert(slot_rows, gate_weight, up_weight, down_weight):
    gate_next = jnp.dot(
        slot_rows,
        lax.all_gather(gate_weight, "wa", axis=0, tiled=True),
        preferred_element_type=jnp.float32,
    )
    up_next = jnp.dot(
        slot_rows,
        lax.all_gather(up_weight, "wa", axis=0, tiled=True),
        preferred_element_type=jnp.float32,
    )
    hidden = (jax.nn.silu(gate_next) * up_next).astype(jnp.bfloat16)
    return lax.dot_general(
        hidden,
        lax.all_gather(down_weight, "wa", axis=0, tiled=True),
        (((1,), (1,)), ((), ())),
        preferred_element_type=jnp.float32,
    )


def per_device(tokens, expert_ids, keep_mask, route_weight, gate_weight, up_weight, down_weight):
    matches = (expert_ids == 0) & (keep_mask == 1)
    chosen = jnp.any(matches, axis=1).astype(jnp.int32)
    route_sum = jnp.sum(jnp.where(matches, route_weight, jnp.float32(0.0)), axis=1)
    position = jnp.cumsum(chosen) - chosen
    admitted = global_admit(chosen, position)
    dispatch = slot_table(position, admitted)
    slot_rows = jnp.dot(
        dispatch.astype(jnp.bfloat16), tokens, preferred_element_type=jnp.float32
    ).astype(jnp.bfloat16)
    expert_out = run_expert(slot_rows, gate_weight, up_weight, down_weight)
    final_table = slot_table(position, admitted)
    combine_map = jnp.where(final_table.T, route_sum[:, None], jnp.float32(0.0))
    halves = lax.psum_scatter(expert_out, "ha", scatter_dimension=1, tiled=True)
    mixed = jnp.dot(
        combine_map, halves, precision=lax.Precision.HIGHEST, preferred_element_type=jnp.float32
    )
    return mixed.astype(jnp.bfloat16)


def solution(mesh):
    return jax.shard_map(
        per_device,
        mesh=mesh,
        in_specs=(
            P("wa", None),
            P("wa", None),
            P("wa", None),
            P("wa", None),
            P("wa", "ha"),
            P("wa", "ha"),
            P("wa", "ha"),
        ),
        out_specs=P("wa", "ha"),
        check_vma=False,
    )
```

profile of v0, /device:TPU:0, one launch (start us, length us, event | category | flops | bytes accessed | tf_op | source)
XLA Modules:
  0.0 254.8 jit_solution(10121087111049697661)
XLA Ops:
  6.5 0.0 all-gather.4.cloned.1.call-start
  6.5 0.7 all-gather.4.cloned.1.call-update
  7.3 0.0 all-gather.6.cloned.1.call-start
  7.3 0.7 all-gather.6.cloned.1.call-update
  8.0 0.0 all-gather.8.cloned.1.call-start
  8.1 0.7 all-gather.8.cloned.1.call-update
  8.7 0.0 reduce-scatter.2.cloned.1.call-start
  8.8 0.8 select_reduce_fusion
  9.6 1.2 dynamic-slice
  10.9 0.7 convert_reduce_fusion
  11.6 1.3 dynamic-update-slice
  12.9 14.4 %all-reduce = s32[16]{0:T(128)S(1)} all-reduce(s32[16]{0:T(128)S(1)} %dynamic-update-slice), channel_id=1, replica_groups=mesh['wa'=16,'ha'=2] {'wa'}, use_global_device_ids=true, to_apply=%add | all-reduce | flops 16 | bytes 128
  27.3 0.3 reduce-window.9
  27.5 0.1 slice.7
  27.6 18.4 %while.13 = (s32[]{:T(128)}, s32[1]{0:T(128)}, s32[]{:T(128)}, s32[16,1]{0,1:T(1,128)S(1)}, s32[]{:T(128)}) while((s32[]{:T(128)}, s32[1]{0:T(128)}, s32[]{:T(128)}, s32[16,1]{0,1:T(1,128)S(1)}, s32[]{:T(128)}) %tuple.41), condition=%wide.region_5.6_spmd, body=%wide.region_4.5_spmd.sunk | while | flops 5 | bytes 107 | solution.py:18
  27.6 0.6 constant_dynamic-slice_fusion.2
  28.9 0.6 constant_dynamic-slice_fusion.2
  30.1 0.6 constant_dynamic-slice_fusion.2
  31.3 0.6 constant_dynamic-slice_fusion.2
  32.6 0.6 constant_dynamic-slice_fusion.2
  33.8 0.6 constant_dynamic-slice_fusion.2
  35.0 0.6 constant_dynamic-slice_fusion.2
  36.3 0.6 constant_dynamic-slice_fusion.2
  37.5 0.6 constant_dynamic-slice_fusion.2
  38.7 0.6 constant_dynamic-slice_fusion.2
  39.9 0.6 constant_dynamic-slice_fusion.2
  41.2 0.6 constant_dynamic-slice_fusion.2
  42.4 0.6 constant_dynamic-slice_fusion.2
  43.6 0.6 constant_dynamic-slice_fusion.2
  44.9 0.6 constant_dynamic-slice_fusion.2
  46.1 0.1 slice_reduce_fusion
  46.2 0.1 fusion.19
  46.3 4.7 %convolution_convert_fusion = bf16[128,4096]{1,0:T(8,128)(2,1)S(1)} fusion(bf16[1024,4096]{1,0:T(8,128)(2,1)} %param.9, s32[1024]{0:T(1024)S(1)} %get-tuple-element.96, pred[1024]{0:T(1024)(128)(4,1)S(1)} %get-tuple-element.95), kind=kOutput, calls=%fused_computation.1 | convolution fusion | flops 1074528256 | bytes 9442304 | tf_op jit(solution)/shard_map/dot_general | solution.py:64
  51.0 22.8 %all-gather.4.cloned.1.call-done = bf16[4096,768]{1,0:T(8,128)(2,1)} async-done(((bf16[256,768]{1,0:T(8,128)(2,1)}), bf16[4096,768]{1,0:T(8,128)(2,1)}) %all-gather.4.cloned.1.call-update) | async-done | bytes 6291472 | tf_op jit(solution)/shard_map/all_gather | solution.py:40
  73.8 3.8 %fusion.22 = f32[128,768]{1,0:T(8,128)S(1)} fusion(bf16[128,4096]{1,0:T(8,128)(2,1)S(1)} %convolution_convert_fusion, bf16[4096,768]{1,0:T(8,128)(2,1)} %all-gather.4.cloned.1.call-done), kind=kOutput, calls=%fused_computation.34 | convolution fusion | flops 805306368 | bytes 7733248 | tf_op jit(solution)/shard_map/dot_general | solution.py:38
  77.6 58.6 %all-gather.6.cloned.1.call-done = bf16[4096,768]{1,0:T(8,128)(2,1)} async-done(((bf16[256,768]{1,0:T(8,128)(2,1)}), bf16[4096,768]{1,0:T(8,128)(2,1)}) %all-gather.6.cloned.1.call-update) | async-done | bytes 6291472 | tf_op jit(solution)/shard_map/all_gather | solution.py:45
  136.2 62.4 %all-gather.8.cloned.1.call-done = bf16[4096,768]{1,0:T(8,128)(2,1)} async-done(((bf16[256,768]{1,0:T(8,128)(2,1)}), bf16[4096,768]{1,0:T(8,128)(2,1)}) %all-gather.8.cloned.1.call-update) | async-done | bytes 6291472 | tf_op jit(solution)/shard_map/all_gather | solution.py:51
  198.7 9.0 %fusion.1 = f32[128,4096]{1,0:T(8,128)} fusion(bf16[4096,768]{1,0:T(8,128)(2,1)} %all-gather.8.cloned.1.call-done, bf16[128,4096]{1,0:T(8,128)(2,1)S(1)} %convolution_convert_fusion, bf16[4096,768]{1,0:T(8,128)(2,1)} %all-gather.6.cloned.1.call-done, f32[128,768]{1,0:T(8,128)S(1)} %fusion.22), kind=kOutput, calls=%fused_computation.5 | convolution fusion | flops 1611202560 | bytes 16121856 | tf_op jit(solution)/shard_map/dot_general | solution.py:49
  207.7 0.0 reduce-scatter.2.cloned.1.call-update
  207.7 30.7 %reduce-scatter.2.cloned.1.call-done = f32[128,2048]{1,0:T(8,128)} async-done(((f32[128,4096]{1,0:T(8,128)}), f32[128,2048]{1,0:T(8,128)}) %reduce-scatter.2.cloned.1.call-update) | async-done | bytes 1048592 | tf_op jit(solution)/shard_map/reduce_scatter | solution.py:70
  238.4 9.9 %convolution_convert_fusion.1 = bf16[1024,2048]{1,0:T(8,128)(2,1)} fusion(f32[128,2048]{1,0:T(8,128)} %reduce-scatter.2.cloned.1.call-done, f32[1024]{0:T(1024)S(1)} %get-tuple-element.93, s32[1024]{0:T(1024)S(1)} %get-tuple-element.96, pred[1024]{0:T(1024)(128)(4,1)S(1)} %get-tuple-element.95), kind=kOutput, calls=%fused_computation.2 | convolution fusion | flops 3223715840 | bytes 5252096 | tf_op jit(solution)/shard_map/dot_general | solution.py:71
  (4 shorter events, 0.1 us)
Async XLA Ops:
  6.5 67.3 %all-gather.4.cloned.1.call-start = ((), (), s32[]{:S(2)}) async-start(), calls=%async_computation.1 | async-start | bytes 6684672 | tf_op jit(solution)/shard_map/all_gather | solution.py:40
  7.3 129.0 %all-gather.6.cloned.1.call-start = ((), (), s32[]{:S(2)}) async-start(), calls=%async_computation.2 | async-start | bytes 6684672 | tf_op jit(solution)/shard_map/all_gather | solution.py:45
  8.0 190.6 %all-gather.8.cloned.1.call-start = ((), (), s32[]{:S(2)}) async-start(), calls=%async_computation.3 | async-start | bytes 6684672 | tf_op jit(solution)/shard_map/all_gather | solution.py:51
  8.7 229.7 %reduce-scatter.2.cloned.1.call-start = ((), (), s32[]{:S(2)}) async-start(), calls=%async_computation.4 | async-start | bytes 3145728 | tf_op jit(solution)/shard_map/reduce_scatter | solution.py:70
Sparse Core Ops, SparseCore 0:
  9.6 64.1 all-gather.3
  76.1 60.0 all-gather.5
  138.5 60.0 all-gather.7
  207.8 30.5 reduce-scatter.1
where the time goes:
time: 255 us
  waiting for transfers between devices  177 us (69%)
  matrix products  27.4 us (11%)
  blocking collectives  14.4 us (6%)
  between operations  13.2 us (5%)
  local copies, waits for them, and re-layouts  11.6 us (5%)
  loops' own time  9.59 us (4%)
    all_gather x1, waiting for transfers between devices, run_expert(): lax.all_gather(down_weight, 'wa', axis=0, tiled=True)  62.4 us
    all_gather x1, waiting for transfers between devices, run_expert(): lax.all_gather(up_weight, 'wa', axis=0, tiled=True)  58.6 us
    reduce_scatter x1, waiting for transfers between devices, per_device(): halves = lax.psum_scatter(expert_out, 'ha', scatter_dimension=1, tiled=True)  30.7 us
    all_gather x1, waiting for transfers between devices, run_expert(): lax.all_gather(gate_weight, 'wa', axis=0, tiled=True)  22.8 us
    unnamed x1, blocking collectives  14.4 us
    dot_general x1, matrix products, per_device(): jnp.dot(combine_map, halves, precision=lax.Precision.HIGHEST, preferred_e...  9.87 us
    another operation x1, loops' own time, prefix(): return lax.fori_loop(0, count - 1, turn, subtotal)  9.59 us
    dot_general x1, matrix products, run_expert(): lax.dot_general(hidden, lax.all_gather(down_weight, 'wa', axis=0, tiled=T...  9.02 us
  transfers between devices with their start and end apart: 4, of which 4 were waited for; matrix products, arithmetic and copies ran while one was open for 9% of the time, Pallas kernels for 0%

commit v1 on v0

--- a/solution.py
+++ b/solution.py
@@ -37,7 +37,9 @@
 def run_expert(slot_rows, gate_weight, up_weight, down_weight):
     gate_next = jnp.dot(
         slot_rows,
-        lax.all_gather(gate_weight, "wa", axis=0, tiled=True),
+        jnp.concatenate(
+            lax.all_to_all(jnp.stack([gate_weight] * lax.axis_size("wa")), "wa", 0, 0), axis=0
+        ),
         preferred_element_type=jnp.float32,
     )
     up_next = jnp.dot(

time: 255 us -> 298 us (1.17)
  blocking collectives: 14.4 us -> 191 us
  waiting for transfers between devices: 177 us -> 33.5 us
  starting transfers between devices: 0.12 us -> 7.68 us
  local copies, waits for them, and re-layouts: 11.6 us -> 14.9 us
    unnamed x1, blocking collectives: 14.4 us -> 191 us
    all_gather x1, waiting for transfers between devices: 62.4 us -> 0.02 us  [run_expert(): lax.all_gather(down_weight, 'wa', axis=0, tiled=True)]
    all_gather x1, waiting for transfers between devices: 58.6 us -> 0.02 us  [run_expert(): lax.all_gather(up_weight, 'wa', axis=0, tiled=True)]
    all_gather x1 -> x0, waiting for transfers between devices: 22.8 us -> none  [run_expert(): lax.all_gather(gate_weight, 'wa', axis=0, tiled=True)]
    all_to_all x0 -> x1, starting transfers between devices: none -> 7.6 us  [run_expert(): lax.all_to_all(jnp.stack([gate_weight] * lax.axis_size('wa')), 'wa', 0, 0)]
    another operation x1 -> x2, local copies, waits for them, and re-layouts: 0.11 us -> 4.32 us  [the longest x1 4.2 us: run_expert(): jnp.stack([gate_weight] * lax.axis_size('wa'))]
  transfers between devices with their start and end apart: 4 -> 4, of which waited for: 4 -> 1; matrix products, arithmetic and copies ran while one was open for 9% -> 8% of each run, Pallas kernels for 0% -> 0%
where the time goes in v1:
time: 298 us
  blocking collectives  191 us (64%)
  waiting for transfers between devices  33.5 us (11%)
  matrix products  27.4 us (9%)
  local copies, waits for them, and re-layouts  14.9 us (5%)
  between operations  13.2 us (4%)
  loops' own time  8.75 us (3%)
  starting transfers between devices  7.68 us (3%)
    unnamed x1, blocking collectives  191 us
    reduce_scatter x1, waiting for transfers between devices, per_device(): halves = lax.psum_scatter(expert_out, 'ha', scatter_dimension=1, tiled=True)  32 us
    dot_general x1, matrix products, per_device(): jnp.dot(combine_map, halves, precision=lax.Precision.HIGHEST, preferred_e...  9.87 us
    dot_general x1, matrix products, run_expert(): lax.dot_general(hidden, lax.all_gather(down_weight, 'wa', axis=0, tiled=T...  9.02 us
    another operation x1, loops' own time, prefix(): return lax.fori_loop(0, count - 1, turn, subtotal)  8.75 us
    dynamic_slice x15, local copies, waits for them, and re-layouts, turn(): longer = join(subtotal, pieces[position])  8.66 us
    all_to_all x1, starting transfers between devices, run_expert(): lax.all_to_all(jnp.stack([gate_weight] * lax.axis_size('wa')), 'wa', 0, 0)  7.6 us
  transfers between devices with their start and end apart: 4, of which 1 were waited for; matrix products, arithmetic and copies ran while one was open for 8% of the time, Pallas kernels for 0%

profile of v1, /device:TPU:0, one launch (start us, length us, event | category | flops | bytes accessed | tf_op | source)
XLA Modules:
  0.0 297.8 jit_solution(1920746839595108730)
XLA Ops:
  6.5 0.0 all-gather.3.cloned.1.call-start
  6.5 0.7 all-gather.3.cloned.1.call-update
  7.3 4.2 %stack.2 = bf16[16,256,768]{2,1,0:T(8,128)(2,1)} broadcast(bf16[256,768]{1,0:T(8,128)(2,1)} %param.13), dimensions={1,2} | broadcast | bytes 6684672 | tf_op jit(solution)/shard_map/stack | solution.py:41
  11.5 0.0 copy-start
  11.5 0.0 copy-start.1
  11.5 0.0 copy-start.2
  11.5 0.0 copy-start.3
  11.5 7.6 %all-to-all-start = ((bf16[16,256,768]{2,1,0:T(8,128)(2,1)}), bf16[16,256,768]{2,1,0:T(8,128)(2,1)}, u32[]{:S(2)}, u32[]{:S(2)}) async-start(bf16[16,256,768]{2,1,0:T(8,128)(2,1)} %stack.2), calls=%async_computation | async-start | bytes 12582912 | tf_op jit(solution)/shard_map/all_to_all | solution.py:41
  19.1 0.0 all-gather.5.cloned.1.call-start
  19.1 0.7 all-gather.5.cloned.1.call-update
  19.8 0.0 reduce-scatter.2.cloned.1.call-start
  19.9 0.0 copy-done
  19.9 0.0 copy-done.1
  19.9 0.0 copy-done.2
  20.0 0.0 copy-done.3
  20.0 0.6 dynamic-slice
  20.6 0.6 convert_reduce_fusion
  21.2 1.3 dynamic-update-slice
  22.5 191.2 %all-reduce = s32[16]{0:T(128)S(1)} all-reduce(s32[16]{0:T(128)S(1)} %dynamic-update-slice), channel_id=1, replica_groups=mesh['wa'=16,'ha'=2] {'wa'}, use_global_device_ids=true, to_apply=%add | all-reduce | flops 16 | bytes 128
  213.7 0.3 reduce-window.9
  214.0 0.1 slice.7
  214.1 17.4 %while.13 = (s32[]{:T(128)}, s32[1]{0:T(128)}, s32[]{:T(128)}, s32[16,1]{0,1:T(1,128)S(1)}, s32[]{:T(128)}) while((s32[]{:T(128)}, s32[1]{0:T(128)}, s32[]{:T(128)}, s32[16,1]{0,1:T(1,128)S(1)}, s32[]{:T(128)}) %tuple.39), condition=%wide.region_5.6_spmd, body=%wide.region_4.5_spmd.sunk | while | flops 5 | bytes 107 | solution.py:18
  214.1 0.6 constant_dynamic-slice_fusion.2
  215.3 0.6 constant_dynamic-slice_fusion.2
  216.4 0.6 constant_dynamic-slice_fusion.2
  217.6 0.6 constant_dynamic-slice_fusion.2
  218.8 0.6 constant_dynamic-slice_fusion.2
  219.9 0.6 constant_dynamic-slice_fusion.2
  221.1 0.6 constant_dynamic-slice_fusion.2
  222.2 0.6 constant_dynamic-slice_fusion.2
  223.4 0.6 constant_dynamic-slice_fusion.2
  224.6 0.6 constant_dynamic-slice_fusion.2
  225.7 0.6 constant_dynamic-slice_fusion.2
  226.9 0.6 constant_dynamic-slice_fusion.2
  228.1 0.6 constant_dynamic-slice_fusion.2
  229.2 0.6 constant_dynamic-slice_fusion.2
  230.4 0.6 constant_dynamic-slice_fusion.2
  231.5 0.1 slice_reduce_fusion
  231.6 0.1 fusion.19
  231.7 4.7 %convolution_convert_fusion = bf16[128,4096]{1,0:T(8,128)(2,1)S(1)} fusion(bf16[1024,4096]{1,0:T(8,128)(2,1)} %param.9, s32[1024]{0:T(1024)S(1)} %get-tuple-element.96, pred[1024]{0:T(1024)(128)(4,1)S(1)} %get-tuple-element.95), kind=kOutput, calls=%fused_computation.1 | convolution fusion | flops 1074528256 | bytes 9442304 | tf_op jit(solution)/shard_map/dot_general | solution.py:66
  236.5 0.0 all-to-all-done
  236.5 3.8 %fusion.22 = f32[128,768]{1,0:T(8,128)S(1)} fusion(bf16[128,4096]{1,0:T(8,128)(2,1)S(1)} %convolution_convert_fusion, bf16[4096,768]{1,0:T(8,128)(2,1)} %bitcast.8), kind=kOutput, calls=%fused_computation.34 | convolution fusion | flops 805306368 | bytes 7733248 | tf_op jit(solution)/shard_map/dot_general | solution.py:38
  240.3 0.0 all-gather.3.cloned.1.call-done
  240.3 0.0 all-gather.5.cloned.1.call-done
  240.4 9.0 %fusion.1 = f32[128,4096]{1,0:T(8,128)} fusion(bf16[4096,768]{1,0:T(8,128)(2,1)} %all-gather.5.cloned.1.call-done, bf16[128,4096]{1,0:T(8,128)(2,1)S(1)} %convolution_convert_fusion, bf16[4096,768]{1,0:T(8,128)(2,1)} %all-gather.3.cloned.1.call-done, f32[128,768]{1,0:T(8,128)S(1)} %fusion.22), kind=kOutput, calls=%fused_computation.5 | convolution fusion | flops 1611202560 | bytes 16121856 | tf_op jit(solution)/shard_map/dot_general | solution.py:51
  249.4 0.0 reduce-scatter.2.cloned.1.call-update
  249.4 32.0 %reduce-scatter.2.cloned.1.call-done = f32[128,2048]{1,0:T(8,128)} async-done(((f32[128,4096]{1,0:T(8,128)}), f32[128,2048]{1,0:T(8,128)}) %reduce-scatter.2.cloned.1.call-update) | async-done | bytes 1048592 | tf_op jit(solution)/shard_map/reduce_scatter | solution.py:72
  281.4 9.9 %convolution_convert_fusion.1 = bf16[1024,2048]{1,0:T(8,128)(2,1)} fusion(f32[128,2048]{1,0:T(8,128)} %reduce-scatter.2.cloned.1.call-done, f32[1024]{0:T(1024)S(1)} %get-tuple-element.93, s32[1024]{0:T(1024)S(1)} %get-tuple-element.96, pred[1024]{0:T(1024)(128)(4,1)S(1)} %get-tuple-element.95), kind=kOutput, calls=%fused_computation.2 | convolution fusion | flops 3223715840 | bytes 5252096 | tf_op jit(solution)/shard_map/dot_general | solution.py:73
  (5 shorter events, 0.1 us)
Async XLA Ops:
  6.5 233.8 %all-gather.3.cloned.1.call-start = ((), (), s32[]{:S(2)}) async-start(), calls=%async_computation.2 | async-start | bytes 6684672 | tf_op jit(solution)/shard_map/all_gather | solution.py:47
  11.5 8.4 %copy-start = (f32[1024,8]{0,1:T(8,128)S(1)}, f32[1024,8]{0,1:T(8,128)}, u32[]{:S(2)}) copy-start(f32[1024,8]{0,1:T(8,128)} %param.12) | copy-start | bytes 98308
  11.5 8.4 %copy-start.1 = (s32[1024,8]{0,1:T(8,128)S(1)}, s32[1024,8]{0,1:T(8,128)}, u32[]{:S(2)}) copy-start(s32[1024,8]{0,1:T(8,128)} %param.11) | copy-start | bytes 98308
  11.5 8.4 %copy-start.2 = (s32[1024,8]{0,1:T(8,128)S(1)}, s32[1024,8]{0,1:T(8,128)}, u32[]{:S(2)}) copy-start(s32[1024,8]{0,1:T(8,128)} %param.10) | copy-start | bytes 98308
  11.5 8.5 %copy-start.3 = (u32[32]{0:T(128)S(1)}, u32[32]{0:T(128)}, u32[]{:S(2)}) copy-start(u32[32]{0:T(128)} %constant.51) | copy-start | bytes 388
  11.5 225.0 %all-to-all-start = ((bf16[16,256,768]{2,1,0:T(8,128)(2,1)}), bf16[16,256,768]{2,1,0:T(8,128)(2,1)}, u32[]{:S(2)}, u32[]{:S(2)}) async-start(bf16[16,256,768]{2,1,0:T(8,128)(2,1)} %stack.2), calls=%async_computation | async-start | bytes 12582912 | tf_op jit(solution)/shard_map/all_to_all | solution.py:41
  19.1 221.3 %all-gather.5.cloned.1.call-start = ((), (), s32[]{:S(2)}) async-start(), calls=%async_computation.3 | async-start | bytes 6684672 | tf_op jit(solution)/shard_map/all_gather | solution.py:53
  19.8 261.6 %reduce-scatter.2.cloned.1.call-start = ((), (), s32[]{:S(2)}) async-start(), calls=%async_computation.4 | async-start | bytes 3145728 | tf_op jit(solution)/shard_map/reduce_scatter | solution.py:72
Sparse Core Ops, SparseCore 0:
  9.6 149.9 all-gather.2
  161.9 75.8 all-gather.4
  249.5 31.8 reduce-scatter.1
